TPU v7x, 32 devices: a whole 2x2x4 slice. The times are simulated.
32 devices in a mesh: lon: 4 (over y, x), lat: 8 (over z, core).
Axes of the slice: x: 2, y: 2, z: 4, core: 2. Of those that a mesh axis runs over, the one named last changes fastest.
Arguments:
- spectrum: float32 [32, 512, 648], P('lon', 'lat'), may hold values from 0.01 to 1
- sea_mask: int32 [32, 512], P('lon', 'lat'), may hold values from 0 to 1, as said below
- ice_flags: int32 [32, 512], P('lon', 'lat'), may hold values 0 or 1
- wind_forcing: float32 [32, 512], P('lon', 'lat'), may hold values from 0.1 to 1.5
- group_speed: float32 [18], replicated, may hold values from 0.3 to 1
- coupling: bfloat16 [648, 648], replicated, may hold values from -0.25 to 0.25
Outputs:
- field: float32 [32, 512, 648], P('lon', 'lat')
Inputs may be any that keep to these rules, and one draw needn't show every extreme that they name: `sea_mask`: each device's block of 8 x 64 cells holds at most 384 sea cells and at least 128; in every draw some block holds exactly 384.
All inputs are finite; a program needn't handle non-finite values. No bound on the sum of `ice_flags` on one device may be relied on, other than what follows from the above.
Results may differ from a plain program's by a relative error of at most 0.00079.
Values sent between devices are 32-bit elements; how exact they have to be, the bound alone decides.
A program may use at most 64 MiB of HBM per device.

v0:
```python
import math

import jax
import jax.numpy as jnp
from jax import lax
from jax.sharding import PartitionSpec as P

DIRS = 36
STEPS = 4


time_step = 0.2
dissipation = 0.5


def extended(value, sides, width, wrap):
    for axis, dim in sides:
        size, length = (lax.axis_size(axis), value.shape[dim])
        up = [(i, (i + 1) % size) for i in range(size if wrap else size - 1)]
        down = [(j, i) for i, j in up]
        last = lax.slice_in_dim(value, length - width, length, axis=dim)
        first = lax.slice_in_dim(value, 0, width, axis=dim)
        before = lax.ppermute(last, axis, up)
        after = lax.ppermute(first, axis, down)
        value = jnp.concatenate([before, value, after], axis=dim)
    return value


def speed_tables(rows, total_rows, group_speed, dirs):
    theta = (jnp.arange(dirs).astype(jnp.float32) + 0.5) * (2.0 * math.pi / dirs)
    latitude = (-60.0 + 120.0 * (rows.astype(jnp.float32) + 0.5) / total_rows) * (math.pi / 180.0)
    scaled = jnp.outer(jnp.cos(theta), group_speed).reshape(-1)
    along_x = (0.225 * scaled)[None, :] / jnp.cos(latitude)[:, None]
    along_y = 0.45 * jnp.outer(jnp.sin(theta), group_speed).reshape(-1)
    return (along_x, along_y)


def upwind(field, west, east, south, north, along_x, along_y):
    speed_x = along_x[None]
    result = (
        field
        - jnp.maximum(speed_x, 0.0) * (field - west)
        - jnp.minimum(speed_x, 0.0) * (east - field)
    )
    return (
        result
        - jnp.maximum(along_y, 0.0) * (field - south)
        - jnp.minimum(along_y, 0.0) * (north - field)
    )


def sources(advected, wind_forcing, ice_flags, coupling):
    shape = advected.shape
    energy = jnp.mean(advected, axis=-1, keepdims=True)
    flat = advected.reshape(-1, shape[-1]).astype(jnp.bfloat16)
    transfer = jnp.dot(flat, coupling, preferred_element_type=jnp.float32).reshape(shape)
    forcing = (wind_forcing * (1.0 - ice_flags.astype(jnp.float32)))[..., None]
    return advected + time_step * (forcing * advected + transfer - dissipation * energy * advected)


def neighbours(field):
    wide_x = extended(field, (("lon", 0),), 1, True)
    wide_y = extended(field, (("lat", 1),), 1, False)
    return (wide_x[:-2], wide_x[2:], wide_y[:, :-2], wide_y[:, 2:])


def on_device(spectrum, sea_mask, ice_flags, wind_forcing, group_speed, coupling):
    rows_here = spectrum.shape[1]
    rows = lax.axis_index("lat") * rows_here + jnp.arange(rows_here, dtype=jnp.int32)
    along_x, along_y = speed_tables(rows, rows_here * lax.axis_size("lat"), group_speed, DIRS)
    sea = sea_mask.astype(jnp.float32)[..., None]
    field = spectrum * sea
    for step in range(STEPS):
        west, east, south, north = neighbours(field)
        advected = upwind(field, west, east, south, north, along_x, along_y)
        field = sources(advected, wind_forcing, ice_flags, coupling) * sea
    return field


def solution(mesh):
    placed = (P("lon", "lat", None), P("lon", "lat"), P("lon", "lat"), P("lon", "lat"), P(), P())
    return jax.shard_map(
        on_device, mesh=mesh, in_specs=placed, out_specs=P("lon", "lat", None), check_vma=False
    )
```

profile of v0, /device:TPU:1, one launch (start us, length us, event | category | flops | bytes accessed | tf_op | source)
XLA Modules:
  0.0 67.7 jit_solution(12144094791909609757)
XLA Ops:
  0.0 0.8 %convert_element_type.44 = f32[8,64]{1,0:T(8,128)S(1)} convert(s32[8,64]{1,0:T(8,128)} %param.7) | non-fusion elementwise | flops 512 | bytes 4096 | tf_op jit(solution)/shard_map/convert_element_type | solution.py:71
  0.8 1.6 %broadcast_multiply_fusion = f32[8,64,648]{2,1,0:T(8,128)S(1)} fusion(f32[8,64,648]{2,1,0:T(8,128)} %param.6, f32[8,64]{1,0:T(8,128)S(1)} %convert_element_type.44), kind=kLoop, calls=%fused_computation.80 | loop fusion | flops 331776 | bytes 2656256 | tf_op jit(solution)/shard_map/mul | solution.py:72
  3.0 4.6 %collective-permute-start.2 = (f32[8,1,648]{2,1,0:T(1,128)}, f32[8,1,648]{2,1,0:T(1,128)}, u32[]{:S(2)}, u32[]{:S(2)}) collective-permute-start(f32[8,1,648]{2,1,0:T(1,128)} %get-tuple-element.27), channel_id=1, source_target_pairs={{0,1},{1,2},{2,3},{3,4},{4,5},{5,6},{6,7},{8,9},{9,10},{10,11},{11... | collective-permute-start | bytes 62216 | tf_op jit(solution)/shard_map/ppermute | solution.py:23
  7.6 1.9 %collective-permute-start.3 = (f32[8,1,648]{2,1,0:T(1,128)}, f32[8,1,648]{2,1,0:T(1,128)}, u32[]{:S(2)}, u32[]{:S(2)}) collective-permute-start(f32[8,1,648]{2,1,0:T(1,128)} %get-tuple-element.28), channel_id=1, source_target_pairs={{1,0},{2,1},{3,2},{4,3},{5,4},{6,5},{7,6},{9,8},{10,9},{11,10},{12... | collective-permute-start | bytes 62216 | tf_op jit(solution)/shard_map/ppermute | solution.py:24
  9.6 0.7 %fusion.94 = (f32[1,64,648]{2,1,0:T(8,128)}, f32[1,64,648]{2,1,0:T(8,128)S(1)}) fusion(f32[8,64,648]{2,1,0:T(8,128)S(1)} %broadcast_multiply_fusion), kind=kLoop, calls=%fused_computation.106 | loop fusion | bytes 663552 | tf_op jit(solution)/shard_map/slice | solution.py:21
  10.3 1.2 %collective-permute-start = (f32[1,64,648]{2,1,0:T(8,128)}, f32[1,64,648]{2,1,0:T(8,128)S(1)}, u32[]{:S(2)}, u32[]{:S(2)}) collective-permute-start(f32[1,64,648]{2,1,0:T(8,128)} %get-tuple-element.25), channel_id=1, source_target_pairs={{0,8},{8,16},{16,24},{24,0},{1,9},{9,17},{17,25},{25,1},{2,10},{10... | collective-permute-start | bytes 497672 | tf_op jit(solution)/shard_map/ppermute | solution.py:23
  11.5 1.2 %collective-permute-start.1 = (f32[1,64,648]{2,1,0:T(8,128)S(1)}, f32[1,64,648]{2,1,0:T(8,128)S(1)}, u32[]{:S(2)}, u32[]{:S(2)}) collective-permute-start(f32[1,64,648]{2,1,0:T(8,128)S(1)} %get-tuple-element.26), channel_id=1, source_target_pairs={{8,0},{16,8},{24,16},{0,24},{9,1},{17,9},{25,17},{1,25},{10,2},{18... | collective-permute-start | bytes 497672 | tf_op jit(solution)/shard_map/ppermute | solution.py:24
  14.7 1.3 %subtract_multiply_fusion = f32[8,64]{1,0:T(8,128)} fusion(f32[8,64]{1,0:T(8,128)} %param.9, s32[8,64]{1,0:T(8,128)} %param.8), kind=kLoop, calls=%fused_computation.87 | loop fusion | flops 1536 | bytes 6144 | tf_op jit(solution)/shard_map/mul | solution.py:57
  16.0 0.8 %max.26 = f32[648]{0:T(1024)S(1)} reshape(f32[36,18]{1,0:T(8,128)} %get-tuple-element.31) | data formatting | bytes 5184 | tf_op jit(solution)/shard_map/max | solution.py:47
  16.9 1.4 %min.26 = f32[648]{0:T(1024)} reshape(f32[36,18]{1,0:T(8,128)} %get-tuple-element.32) | data formatting | bytes 5184 | tf_op jit(solution)/shard_map/min | solution.py:48
  18.3 3.0 %collective-permute-done.1 = f32[1,64,648]{2,1,0:T(8,128)S(1)} collective-permute-done((f32[1,64,648]{2,1,0:T(8,128)S(1)}, f32[1,64,648]{2,1,0:T(8,128)S(1)}, u32[]{:S(2)}, u32[]{:S(2)}) %collective-permute-start.1) | collective-permute-done | bytes 165920 | tf_op jit(solution)/shard_map/ppermute | solution.py:24
  21.3 1.8 %fusion.86 = (f32[8,64]{1,0:T(8,128)S(1)}, f32[8,64,648]{2,1,0:T(8,128)S(1)}) fusion(f32[8,64,648]{2,1,0:T(8,128)S(1)} %broadcast_multiply_fusion, f32[8,1,648]{2,1,0:T(1,128)} %collective-permute-done.3, f32[648]{0:T(1024)} %min.26, f32[8,1,648]{2,1,0:T(1,128)} %collective-permute-done.2, f32[648]{0:T(1024)S(1)} %max.26, ...), kind=kLoop, calls=%fused_computation.99 | loop fusion | flops 5639680 | bytes 3366464 | tf_op jit(solution)/shard_map/reduce_sum | solution.py:54
  23.2 1.0 %add_multiply_fusion.3 = f32[8,64,648]{2,1,0:T(8,128)S(1)} fusion(f32[8,64,648]{2,1,0:T(8,128)S(1)} %get-tuple-element.12, f32[8,64]{1,0:T(8,128)S(1)} %broadcast_multiply_fusion.4, bf16[648,648]{1,0:T(8,128)(2,1)S(1)} %copy-done, f32[8,64]{1,0:T(8,128)S(1)} %copy-done.4, f32[8,64]{1,0:T(8,128)S(1)} %copy-done.3), kind=kOutput, calls=%fused_computation.67 | convolution fusion | flops 432635904 | bytes 3500160 | tf_op jit(solution)/shard_map/dot_general | solution.py:56
  24.3 1.3 %collective-permute-start.4 = (f32[1,64,648]{2,1,0:T(8,128)S(1)}, f32[1,64,648]{2,1,0:T(8,128)S(1)}, u32[]{:S(2)}, u32[]{:S(2)}) collective-permute-start(f32[1,64,648]{2,1,0:T(8,128)S(1)} %get-tuple-element.21), channel_id=1, source_target_pairs={{0,8},{8,16},{16,24},{24,0},{1,9},{9,17},{17,25},{25,1},{2,10},{10... | collective-permute-start | bytes 497672 | tf_op jit(solution)/shard_map/ppermute | solution.py:23
  25.5 1.2 %collective-permute-start.5 = (f32[1,64,648]{2,1,0:T(8,128)S(1)}, f32[1,64,648]{2,1,0:T(8,128)S(1)}, u32[]{:S(2)}, u32[]{:S(2)}) collective-permute-start(f32[1,64,648]{2,1,0:T(8,128)S(1)} %get-tuple-element.22), channel_id=1, source_target_pairs={{8,0},{16,8},{24,16},{0,24},{9,1},{17,9},{25,17},{1,25},{10,2},{18... | collective-permute-start | bytes 497672 | tf_op jit(solution)/shard_map/ppermute | solution.py:24
  26.7 5.3 %collective-permute-start.6 = (f32[8,1,648]{2,1,0:T(1,128)S(1)}, f32[8,1,648]{2,1,0:T(1,128)S(1)}, u32[]{:S(2)}, u32[]{:S(2)}) collective-permute-start(f32[8,1,648]{2,1,0:T(1,128)S(1)} %get-tuple-element.23), channel_id=1, source_target_pairs={{0,1},{1,2},{2,3},{3,4},{4,5},{5,6},{6,7},{8,9},{9,10},{10,11},{11... | collective-permute-start | bytes 62216 | tf_op jit(solution)/shard_map/ppermute | solution.py:23
  32.0 1.9 %collective-permute-start.7 = (f32[8,1,648]{2,1,0:T(1,128)S(1)}, f32[8,1,648]{2,1,0:T(1,128)S(1)}, u32[]{:S(2)}, u32[]{:S(2)}) collective-permute-start(f32[8,1,648]{2,1,0:T(1,128)S(1)} %get-tuple-element.24), channel_id=1, source_target_pairs={{1,0},{2,1},{3,2},{4,3},{5,4},{6,5},{7,6},{9,8},{10,9},{11,10},{12... | collective-permute-start | bytes 62216 | tf_op jit(solution)/shard_map/ppermute | solution.py:24
  33.9 3.2 %collective-permute-done.7 = f32[8,1,648]{2,1,0:T(1,128)S(1)} collective-permute-done((f32[8,1,648]{2,1,0:T(1,128)S(1)}, f32[8,1,648]{2,1,0:T(1,128)S(1)}, u32[]{:S(2)}, u32[]{:S(2)}) %collective-permute-start.7) | collective-permute-done | bytes 20768 | tf_op jit(solution)/shard_map/ppermute | solution.py:24
  37.2 1.1 %fusion.84 = (f32[8,64]{1,0:T(8,128)S(1)}, f32[8,64,648]{2,1,0:T(8,128)S(1)}) fusion(f32[8,64,648]{2,1,0:T(8,128)S(1)} %add_multiply_fusion.3, f32[8,1,648]{2,1,0:T(1,128)S(1)} %collective-permute-done.7, f32[648]{0:T(1024)S(1)} %copy-done.1, f32[8,1,648]{2,1,0:T(1,128)S(1)} %collective-permute-done.6, f32[648]{0:T(1024)S(1)} %max.26, ...), kind=kLoop, calls=%fused_computation.98 | loop fusion | flops 5639680 | bytes 3366464 | tf_op jit(solution)/shard_map/reduce_sum | solution.py:54
  38.3 1.0 %add_multiply_fusion.2 = f32[8,64,648]{2,1,0:T(8,128)S(1)} fusion(f32[8,64,648]{2,1,0:T(8,128)S(1)} %get-tuple-element.10, f32[8,64]{1,0:T(8,128)S(1)} %broadcast_multiply_fusion.3, bf16[648,648]{1,0:T(8,128)(2,1)S(1)} %copy-done, f32[8,64]{1,0:T(8,128)S(1)} %copy-done.4, f32[8,64]{1,0:T(8,128)S(1)} %copy-done.3), kind=kOutput, calls=%fused_computation.66 | convolution fusion | flops 432635904 | bytes 3500160 | tf_op jit(solution)/shard_map/dot_general | solution.py:56
  39.7 2.1 %collective-permute-start.9 = (f32[1,64,648]{2,1,0:T(8,128)S(1)}, f32[1,64,648]{2,1,0:T(8,128)S(1)}, u32[]{:S(2)}, u32[]{:S(2)}) collective-permute-start(f32[1,64,648]{2,1,0:T(8,128)S(1)} %get-tuple-element.18), channel_id=1, source_target_pairs={{8,0},{16,8},{24,16},{0,24},{9,1},{17,9},{25,17},{1,25},{10,2},{18... | collective-permute-start | bytes 497672 | tf_op jit(solution)/shard_map/ppermute | solution.py:24
  41.8 2.5 %collective-permute-start.10 = (f32[8,1,648]{2,1,0:T(1,128)S(1)}, f32[8,1,648]{2,1,0:T(1,128)S(1)}, u32[]{:S(2)}, u32[]{:S(2)}) collective-permute-start(f32[8,1,648]{2,1,0:T(1,128)S(1)} %get-tuple-element.19), channel_id=1, source_target_pairs={{0,1},{1,2},{2,3},{3,4},{4,5},{5,6},{6,7},{8,9},{9,10},{10,11},{11... | collective-permute-start | bytes 62216 | tf_op jit(solution)/shard_map/ppermute | solution.py:23
  44.3 1.9 %collective-permute-start.11 = (f32[8,1,648]{2,1,0:T(1,128)S(1)}, f32[8,1,648]{2,1,0:T(1,128)S(1)}, u32[]{:S(2)}, u32[]{:S(2)}) collective-permute-start(f32[8,1,648]{2,1,0:T(1,128)S(1)} %get-tuple-element.20), channel_id=1, source_target_pairs={{1,0},{2,1},{3,2},{4,3},{5,4},{6,5},{7,6},{9,8},{10,9},{11,10},{12... | collective-permute-start | bytes 62216 | tf_op jit(solution)/shard_map/ppermute | solution.py:24
  46.3 3.5 %collective-permute-done.11 = f32[8,1,648]{2,1,0:T(1,128)S(1)} collective-permute-done((f32[8,1,648]{2,1,0:T(1,128)S(1)}, f32[8,1,648]{2,1,0:T(1,128)S(1)}, u32[]{:S(2)}, u32[]{:S(2)}) %collective-permute-start.11) | collective-permute-done | bytes 20768 | tf_op jit(solution)/shard_map/ppermute | solution.py:24
  50.4 1.1 %fusion.82 = (f32[8,64]{1,0:T(8,128)S(1)}, f32[8,64,648]{2,1,0:T(8,128)S(1)}) fusion(f32[8,64,648]{2,1,0:T(8,128)S(1)} %add_multiply_fusion.2, f32[8,1,648]{2,1,0:T(1,128)S(1)} %collective-permute-done.11, f32[648]{0:T(1024)S(1)} %copy-done.1, f32[8,1,648]{2,1,0:T(1,128)S(1)} %collective-permute-done.10, f32[648]{0:T(1024)S(1)} %max.26, ...), kind=kLoop, calls=%fused_computation.97 | loop fusion | flops 5639680 | bytes 3366464 | tf_op jit(solution)/shard_map/reduce_sum | solution.py:54
  51.5 1.0 %add_multiply_fusion.1 = f32[8,64,648]{2,1,0:T(8,128)S(1)} fusion(f32[8,64,648]{2,1,0:T(8,128)S(1)} %get-tuple-element.8, f32[8,64]{1,0:T(8,128)S(1)} %broadcast_multiply_fusion.2, bf16[648,648]{1,0:T(8,128)(2,1)S(1)} %copy-done, f32[8,64]{1,0:T(8,128)S(1)} %copy-done.4, f32[8,64]{1,0:T(8,128)S(1)} %copy-done.3), kind=kOutput, calls=%fused_computation.65 | convolution fusion | flops 432635904 | bytes 3500160 | tf_op jit(solution)/shard_map/dot_general | solution.py:56
  52.7 2.4 %collective-permute-start.13 = (f32[1,64,648]{2,1,0:T(8,128)S(1)}, f32[1,64,648]{2,1,0:T(8,128)S(1)}, u32[]{:S(2)}, u32[]{:S(2)}) collective-permute-start(f32[1,64,648]{2,1,0:T(8,128)S(1)} %get-tuple-element.14), channel_id=1, source_target_pairs={{8,0},{16,8},{24,16},{0,24},{9,1},{17,9},{25,17},{1,25},{10,2},{18... | collective-permute-start | bytes 497672 | tf_op jit(solution)/shard_map/ppermute | solution.py:24
  55.1 4.1 %collective-permute-start.14 = (f32[8,1,648]{2,1,0:T(1,128)S(1)}, f32[8,1,648]{2,1,0:T(1,128)S(1)}, u32[]{:S(2)}, u32[]{:S(2)}) collective-permute-start(f32[8,1,648]{2,1,0:T(1,128)S(1)} %get-tuple-element.15), channel_id=1, source_target_pairs={{0,1},{1,2},{2,3},{3,4},{4,5},{5,6},{6,7},{8,9},{9,10},{10,11},{11... | collective-permute-start | bytes 62216 | tf_op jit(solution)/shard_map/ppermute | solution.py:23
  59.2 1.9 %collective-permute-start.15 = (f32[8,1,648]{2,1,0:T(1,128)S(1)}, f32[8,1,648]{2,1,0:T(1,128)S(1)}, u32[]{:S(2)}, u32[]{:S(2)}) collective-permute-start(f32[8,1,648]{2,1,0:T(1,128)S(1)} %get-tuple-element.16), channel_id=1, source_target_pairs={{1,0},{2,1},{3,2},{4,3},{5,4},{6,5},{7,6},{9,8},{10,9},{11,10},{12... | collective-permute-start | bytes 62216 | tf_op jit(solution)/shard_map/ppermute | solution.py:24
  61.2 3.2 %collective-permute-done.15 = f32[8,1,648]{2,1,0:T(1,128)S(1)} collective-permute-done((f32[8,1,648]{2,1,0:T(1,128)S(1)}, f32[8,1,648]{2,1,0:T(1,128)S(1)}, u32[]{:S(2)}, u32[]{:S(2)}) %collective-permute-start.15) | collective-permute-done | bytes 20768 | tf_op jit(solution)/shard_map/ppermute | solution.py:24
  64.4 1.1 %fusion.80 = (f32[8,64]{1,0:T(8,128)S(1)}, f32[8,64,648]{2,1,0:T(8,128)S(1)}) fusion(f32[8,64,648]{2,1,0:T(8,128)S(1)} %add_multiply_fusion.1, f32[8,1,648]{2,1,0:T(1,128)S(1)} %collective-permute-done.15, f32[648]{0:T(1024)S(1)} %copy-done.1, f32[8,1,648]{2,1,0:T(1,128)S(1)} %collective-permute-done.14, f32[648]{0:T(1024)S(1)} %max.26, ...), kind=kLoop, calls=%fused_computation.96 | loop fusion | flops 5639680 | bytes 3366464 | tf_op jit(solution)/shard_map/reduce_sum | solution.py:54
  65.5 2.2 %add_multiply_fusion = f32[8,64,648]{2,1,0:T(8,128)} fusion(f32[8,64,648]{2,1,0:T(8,128)S(1)} %get-tuple-element.6, f32[8,64]{1,0:T(8,128)S(1)} %broadcast_multiply_fusion.1, bf16[648,648]{1,0:T(8,128)(2,1)S(1)} %copy-done, f32[8,64]{1,0:T(8,128)S(1)} %copy-done.4, f32[8,64]{1,0:T(8,128)S(1)} %copy-done.3), kind=kOutput, calls=%fused_computation.64 | convolution fusion | flops 432635904 | bytes 3500160 | tf_op jit(solution)/shard_map/dot_general | solution.py:56
  (42 shorter events, 4.1 us)
Async XLA Ops:
  0.0 23.2 %copy-start = (bf16[648,648]{1,0:T(8,128)(2,1)S(1)}, bf16[648,648]{1,0:T(8,128)(2,1)}, u32[]{:S(2)}) copy-start(bf16[648,648]{1,0:T(8,128)(2,1)} %param.11) | copy-start | bytes 2519428
  0.8 1.6 %copy-start.2 = (f32[8,64]{1,0:T(8,128)}, f32[8,64]{1,0:T(8,128)S(1)}, u32[]{:S(2)}) copy-start(f32[8,64]{1,0:T(8,128)S(1)} %convert_element_type.44) | copy-start | bytes 6148
  0.8 12.4 %copy-start.5 = (f32[18]{0:T(128)S(1)}, f32[18]{0:T(128)}, u32[]{:S(2)}) copy-start(f32[18]{0:T(128)} %param.10) | copy-start | bytes 220
  3.0 15.2 %collective-permute-start.2 = (f32[8,1,648]{2,1,0:T(1,128)}, f32[8,1,648]{2,1,0:T(1,128)}, u32[]{:S(2)}, u32[]{:S(2)}) collective-permute-start(f32[8,1,648]{2,1,0:T(1,128)} %get-tuple-element.27), channel_id=1, source_target_pairs={{0,1},{1,2},{2,3},{3,4},{4,5},{5,6},{6,7},{8,9},{9,10},{10,11},{11... | collective-permute-start | bytes 62216 | tf_op jit(solution)/shard_map/ppermute | solution.py:23
  7.6 10.7 %collective-permute-start.3 = (f32[8,1,648]{2,1,0:T(1,128)}, f32[8,1,648]{2,1,0:T(1,128)}, u32[]{:S(2)}, u32[]{:S(2)}) collective-permute-start(f32[8,1,648]{2,1,0:T(1,128)} %get-tuple-element.28), channel_id=1, source_target_pairs={{1,0},{2,1},{3,2},{4,3},{5,4},{6,5},{7,6},{9,8},{10,9},{11,10},{12... | collective-permute-start | bytes 62216 | tf_op jit(solution)/shard_map/ppermute | solution.py:24
  10.3 8.0 %collective-permute-start = (f32[1,64,648]{2,1,0:T(8,128)}, f32[1,64,648]{2,1,0:T(8,128)S(1)}, u32[]{:S(2)}, u32[]{:S(2)}) collective-permute-start(f32[1,64,648]{2,1,0:T(8,128)} %get-tuple-element.25), channel_id=1, source_target_pairs={{0,8},{8,16},{16,24},{24,0},{1,9},{9,17},{17,25},{25,1},{2,10},{10... | collective-permute-start | bytes 497672 | tf_op jit(solution)/shard_map/ppermute | solution.py:23
  11.5 9.9 %collective-permute-start.1 = (f32[1,64,648]{2,1,0:T(8,128)S(1)}, f32[1,64,648]{2,1,0:T(8,128)S(1)}, u32[]{:S(2)}, u32[]{:S(2)}) collective-permute-start(f32[1,64,648]{2,1,0:T(8,128)S(1)} %get-tuple-element.26), channel_id=1, source_target_pairs={{8,0},{16,8},{24,16},{0,24},{9,1},{17,9},{25,17},{1,25},{10,2},{18... | collective-permute-start | bytes 497672 | tf_op jit(solution)/shard_map/ppermute | solution.py:24
  21.3 1.8 %copy-start.3 = (f32[8,64]{1,0:T(8,128)S(1)}, f32[8,64]{1,0:T(8,128)}, u32[]{:S(2)}) copy-start(f32[8,64]{1,0:T(8,128)} %copy-done.2) | copy-start | bytes 6148
  21.3 1.8 %copy-start.4 = (f32[8,64]{1,0:T(8,128)S(1)}, f32[8,64]{1,0:T(8,128)}, u32[]{:S(2)}) copy-start(f32[8,64]{1,0:T(8,128)} %subtract_multiply_fusion) | copy-start | bytes 6148
  23.2 14.0 %copy-start.1 = (f32[648]{0:T(1024)S(1)}, f32[648]{0:T(1024)}, u32[]{:S(2)}) copy-start(f32[648]{0:T(1024)} %min.26) | copy-start | bytes 7780
  24.3 12.9 %collective-permute-start.4 = (f32[1,64,648]{2,1,0:T(8,128)S(1)}, f32[1,64,648]{2,1,0:T(8,128)S(1)}, u32[]{:S(2)}, u32[]{:S(2)}) collective-permute-start(f32[1,64,648]{2,1,0:T(8,128)S(1)} %get-tuple-element.21), channel_id=1, source_target_pairs={{0,8},{8,16},{16,24},{24,0},{1,9},{9,17},{17,25},{25,1},{2,10},{10... | collective-permute-start | bytes 497672 | tf_op jit(solution)/shard_map/ppermute | solution.py:23
  25.5 11.6 %collective-permute-start.5 = (f32[1,64,648]{2,1,0:T(8,128)S(1)}, f32[1,64,648]{2,1,0:T(8,128)S(1)}, u32[]{:S(2)}, u32[]{:S(2)}) collective-permute-start(f32[1,64,648]{2,1,0:T(8,128)S(1)} %get-tuple-element.22), channel_id=1, source_target_pairs={{8,0},{16,8},{24,16},{0,24},{9,1},{17,9},{25,17},{1,25},{10,2},{18... | collective-permute-start | bytes 497672 | tf_op jit(solution)/shard_map/ppermute | solution.py:24
  26.7 7.2 %collective-permute-start.6 = (f32[8,1,648]{2,1,0:T(1,128)S(1)}, f32[8,1,648]{2,1,0:T(1,128)S(1)}, u32[]{:S(2)}, u32[]{:S(2)}) collective-permute-start(f32[8,1,648]{2,1,0:T(1,128)S(1)} %get-tuple-element.23), channel_id=1, source_target_pairs={{0,1},{1,2},{2,3},{3,4},{4,5},{5,6},{6,7},{8,9},{9,10},{10,11},{11... | collective-permute-start | bytes 62216 | tf_op jit(solution)/shard_map/ppermute | solution.py:23
  32.0 5.1 %collective-permute-start.7 = (f32[8,1,648]{2,1,0:T(1,128)S(1)}, f32[8,1,648]{2,1,0:T(1,128)S(1)}, u32[]{:S(2)}, u32[]{:S(2)}) collective-permute-start(f32[8,1,648]{2,1,0:T(1,128)S(1)} %get-tuple-element.24), channel_id=1, source_target_pairs={{1,0},{2,1},{3,2},{4,3},{5,4},{6,5},{7,6},{9,8},{10,9},{11,10},{12... | collective-permute-start | bytes 62216 | tf_op jit(solution)/shard_map/ppermute | solution.py:24
  39.4 10.4 %collective-permute-start.8 = (f32[1,64,648]{2,1,0:T(8,128)S(1)}, f32[1,64,648]{2,1,0:T(8,128)S(1)}, u32[]{:S(2)}, u32[]{:S(2)}) collective-permute-start(f32[1,64,648]{2,1,0:T(8,128)S(1)} %get-tuple-element.17), channel_id=1, source_target_pairs={{0,8},{8,16},{16,24},{24,0},{1,9},{9,17},{17,25},{25,1},{2,10},{10... | collective-permute-start | bytes 497672 | tf_op jit(solution)/shard_map/ppermute | solution.py:23
  39.7 10.7 %collective-permute-start.9 = (f32[1,64,648]{2,1,0:T(8,128)S(1)}, f32[1,64,648]{2,1,0:T(8,128)S(1)}, u32[]{:S(2)}, u32[]{:S(2)}) collective-permute-start(f32[1,64,648]{2,1,0:T(8,128)S(1)} %get-tuple-element.18), channel_id=1, source_target_pairs={{8,0},{16,8},{24,16},{0,24},{9,1},{17,9},{25,17},{1,25},{10,2},{18... | collective-permute-start | bytes 497672 | tf_op jit(solution)/shard_map/ppermute | solution.py:24
  41.8 4.4 %collective-permute-start.10 = (f32[8,1,648]{2,1,0:T(1,128)S(1)}, f32[8,1,648]{2,1,0:T(1,128)S(1)}, u32[]{:S(2)}, u32[]{:S(2)}) collective-permute-start(f32[8,1,648]{2,1,0:T(1,128)S(1)} %get-tuple-element.19), channel_id=1, source_target_pairs={{0,1},{1,2},{2,3},{3,4},{4,5},{5,6},{6,7},{8,9},{9,10},{10,11},{11... | collective-permute-start | bytes 62216 | tf_op jit(solution)/shard_map/ppermute | solution.py:23
  44.3 5.4 %collective-permute-start.11 = (f32[8,1,648]{2,1,0:T(1,128)S(1)}, f32[8,1,648]{2,1,0:T(1,128)S(1)}, u32[]{:S(2)}, u32[]{:S(2)}) collective-permute-start(f32[8,1,648]{2,1,0:T(1,128)S(1)} %get-tuple-element.20), channel_id=1, source_target_pairs={{1,0},{2,1},{3,2},{4,3},{5,4},{6,5},{7,6},{9,8},{10,9},{11,10},{12... | collective-permute-start | bytes 62216 | tf_op jit(solution)/shard_map/ppermute | solution.py:24
  52.6 11.7 %collective-permute-start.12 = (f32[1,64,648]{2,1,0:T(8,128)S(1)}, f32[1,64,648]{2,1,0:T(8,128)S(1)}, u32[]{:S(2)}, u32[]{:S(2)}) collective-permute-start(f32[1,64,648]{2,1,0:T(8,128)S(1)} %get-tuple-element.13), channel_id=1, source_target_pairs={{0,8},{8,16},{16,24},{24,0},{1,9},{9,17},{17,25},{25,1},{2,10},{10... | collective-permute-start | bytes 497672 | tf_op jit(solution)/shard_map/ppermute | solution.py:23
  52.7 11.7 %collective-permute-start.13 = (f32[1,64,648]{2,1,0:T(8,128)S(1)}, f32[1,64,648]{2,1,0:T(8,128)S(1)}, u32[]{:S(2)}, u32[]{:S(2)}) collective-permute-start(f32[1,64,648]{2,1,0:T(8,128)S(1)} %get-tuple-element.14), channel_id=1, source_target_pairs={{8,0},{16,8},{24,16},{0,24},{9,1},{17,9},{25,17},{1,25},{10,2},{18... | collective-permute-start | bytes 497672 | tf_op jit(solution)/shard_map/ppermute | solution.py:24
  55.1 6.1 %collective-permute-start.14 = (f32[8,1,648]{2,1,0:T(1,128)S(1)}, f32[8,1,648]{2,1,0:T(1,128)S(1)}, u32[]{:S(2)}, u32[]{:S(2)}) collective-permute-start(f32[8,1,648]{2,1,0:T(1,128)S(1)} %get-tuple-element.15), channel_id=1, source_target_pairs={{0,1},{1,2},{2,3},{3,4},{4,5},{5,6},{6,7},{8,9},{9,10},{10,11},{11... | collective-permute-start | bytes 62216 | tf_op jit(solution)/shard_map/ppermute | solution.py:23
  59.2 5.1 %collective-permute-start.15 = (f32[8,1,648]{2,1,0:T(1,128)S(1)}, f32[8,1,648]{2,1,0:T(1,128)S(1)}, u32[]{:S(2)}, u32[]{:S(2)}) collective-permute-start(f32[8,1,648]{2,1,0:T(1,128)S(1)} %get-tuple-element.16), channel_id=1, source_target_pairs={{1,0},{2,1},{3,2},{4,3},{5,4},{6,5},{7,6},{9,8},{10,9},{11,10},{12... | collective-permute-start | bytes 62216 | tf_op jit(solution)/shard_map/ppermute | solution.py:24
where the time goes:
time: 68.2 us; the launch traced here: 67.7 us
  starting transfers between devices  33.8 us (50%)
  waiting for transfers between devices  13.6 us (20%)
  other arithmetic  10.8 us (16%)
  matrix products  5.26 us (8%)
  local copies, waits for them, and re-layouts  3.92 us (6%)
    ppermute x8, starting transfers between devices, extended(): before = lax.ppermute(last, axis, up)  19.4 us
    ppermute x8, starting transfers between devices, extended(): after = lax.ppermute(first, axis, down)  14.4 us
    ppermute x8, waiting for transfers between devices, extended(): after = lax.ppermute(first, axis, down)  13.6 us
    dot_general x4, matrix products, sources(): jnp.dot(flat, coupling, preferred_element_type=jnp.float32).reshape(shape)  5.26 us
    reduce_sum x4, other arithmetic, sources(): energy = jnp.mean(advected, axis=-1, keepdims=True)  5.15 us
    mul x1, other arithmetic, on_device(): field = spectrum * sea  1.59 us
    slice x8, local copies, waits for them, and re-layouts, extended(): last = lax.slice_in_dim(value, length - width, length, axis=dim)  1.55 us
    min x1, local copies, waits for them, and re-layouts, upwind(): jnp.minimum(along_y, 0.0) * (north - field)  1.43 us
  transfers between devices with their start and end apart: 16, of which 5 were waited for; matrix products, arithmetic and copies ran while one was open for 10% of the time, Pallas kernels for 0%

commit v1 on v0

v1 whole, which is shorter than its diff:
```python
import functools
import math

import jax
import jax.numpy as jnp
from jax import lax
from jax.experimental import pallas as pl
from jax.experimental.pallas import tpu as pltpu
from jax.sharding import PartitionSpec as P

DIRS = 36
STEPS = 4
LANES = 128
PAD = 8
CHUNKS = 2
SHIFT = 40
MESH = pl.DeviceIdType.MESH

time_step = 0.2
dissipation = 0.5


def kernel(
    freqs, speed_ref, sea_ref, ice_ref, wind_ref, spectrum_ref, coupling_ref, out_ref,
    field, staged, weights, raw_weights, rounded, keep_x, push_x, push_y, grow, scale,
    east_out, east_in, west_out, west_in, north_out, north_in, south_out, south_in,
    load_sem, weight_sem, store_sem, lon_send, lon_recv, lat_send, lat_recv,
):
    columns, rows, bins = staged.shape
    tiles = field.shape[2]
    piece = rows // CHUNKS
    mean_of = 1.0 / bins
    quarter, half, late = DIRS // 4 * freqs, DIRS // 2 * freqs, DIRS * 3 // 4 * freqs
    cut_w, cut_y, cut_e = quarter - LANES, half - 2 * LANES, late - 3 * LANES
    tail = bins - (tiles - 1) * LANES

    lon, lat = lax.axis_index("lon"), lax.axis_index("lat")
    lons, lats = lax.axis_size("lon"), lax.axis_size("lat")
    east, west = lax.rem(lon + 1, lons), lax.rem(lon + lons - 1, lons)
    has_south, has_north = lat > 0, lat < lats - 1

    def width(t):
        return LANES if t < tiles - 1 else tail

    order = [0, columns - 1] + list(range(1, columns - 1))
    loads = {
        c: pltpu.make_async_copy(spectrum_ref.at[c], staged.at[c], load_sem.at[c]) for c in order
    }
    for c in order:
        loads[c].start()
    weight_load = pltpu.make_async_copy(coupling_ref, raw_weights, weight_sem)
    weight_load.start()

    barrier = pltpu.get_barrier_semaphore()
    pl.semaphore_signal(barrier, inc=1, device_id=(east, lat), device_id_type=MESH)
    pl.semaphore_signal(barrier, inc=1, device_id=(west, lat), device_id_type=MESH)

    @pl.when(has_south)
    def _():
        pl.semaphore_signal(barrier, inc=1, device_id=(lon, lat - 1), device_id_type=MESH)

    @pl.when(has_north)
    def _():
        pl.semaphore_signal(barrier, inc=1, device_id=(lon, lat + 1), device_id_type=MESH)

    sea = sea_ref[...].astype(jnp.float32)
    forcing = wind_ref[...] * (1.0 - ice_ref[...].astype(jnp.float32))
    growth = jnp.transpose(sea * (1.0 + time_step * forcing))
    sea_rows = jnp.transpose(sea)
    for c in range(columns):
        grow[c] = jnp.broadcast_to(growth[:, c : c + 1], (rows, LANES))
        scale[c] = jnp.broadcast_to(sea_rows[:, c : c + 1], (rows, LANES))

    lane = lax.broadcasted_iota(jnp.int32, (8, LANES), 1)
    lane_piece = lax.broadcasted_iota(jnp.int32, (piece, LANES), 1)
    row = lax.broadcasted_iota(jnp.int32, (rows, LANES), 0) + lat * rows
    latitude = (-60.0 + 120.0 * (row.astype(jnp.float32) + 0.5) / (rows * lats)) * (math.pi / 180.0)
    inverse = 1.0 / jnp.cos(latitude)
    for t in range(tiles):
        number = (lane + t * LANES).astype(jnp.float32)
        direction = jnp.floor((number + 0.5) * (1.0 / freqs))
        freq = number - direction * freqs
        speed = jnp.zeros((8, LANES), jnp.float32)
        for f in range(freqs):
            speed = jnp.where(freq == f, speed_ref[f], speed)
        inside = (lane + t * LANES) < bins
        theta = (direction + 0.5) * (2.0 * math.pi / DIRS)
        along_y = jnp.where(inside, jnp.abs(0.45 * jnp.sin(theta) * speed), 0.0)
        along_x = jnp.where(inside, jnp.abs(0.225 * jnp.cos(theta) * speed), 0.0)
        push_y[t] = along_y
        along_x = along_x[0:1] * inverse
        push_x[t] = along_x
        keep_x[t] = 1.0 - along_x - along_y[0:1]

    zero_row = jnp.zeros((1, LANES), jnp.float32)
    for c in range(columns):
        for t in range(tiles):
            for b in range(2):
                field[b, c, t, PAD - 1 : PAD, :] = zero_row
                field[b, c, t, PAD + rows : PAD + rows + 1, :] = zero_row
        field[0, c, tiles - 1, PAD : PAD + rows, :] = jnp.zeros((rows, LANES), jnp.float32)

    def lon_copy(step, side, k):
        span = pl.ds(k * piece, piece)
        out_buf, in_buf, to = ((east_out, west_in, east), (west_out, east_in, west))[side]
        return pltpu.make_async_remote_copy(
            src_ref=out_buf.at[step, :, span, :],
            dst_ref=in_buf.at[step, :, span, :],
            send_sem=lon_send.at[step, side, k],
            recv_sem=lon_recv.at[step, side, k],
            device_id=(to, lat),
            device_id_type=MESH,
        )

    def lat_copy(step, side):
        out_buf, in_buf, to = ((north_out, south_in, lat + 1), (south_out, north_in, lat - 1))[side]
        return pltpu.make_async_remote_copy(
            src_ref=out_buf.at[step],
            dst_ref=in_buf.at[step],
            send_sem=lat_send.at[step, side],
            recv_sem=lat_recv.at[step, side],
            device_id=(lon, to),
            device_id_type=MESH,
        )

    def send_lon(step, k):
        b = step % 2
        span = slice(k * piece, (k + 1) * piece)
        at = slice(PAD + k * piece, PAD + (k + 1) * piece)
        last = columns - 1
        east_out[step, 0, span, :] = field[b, last, 0, at, :]
        end = pltpu.roll(field[b, last, 5, at, :], SHIFT, 1)
        mixed = jnp.where(lane_piece < cut_w, field[b, last, 1, at, :], end)
        east_out[step, 1, span, :] = jnp.where(lane_piece < cut_e, mixed, field[b, last, 3, at, :])
        east_out[step, 2, span, :] = field[b, last, 4, at, :]
        for i in range(3):
            west_out[step, i, span, :] = field[b, 0, i + 1, at, :]
        lon_copy(step, 0, k).start()
        lon_copy(step, 1, k).start()

    def send_north(step):
        b = step % 2
        low = lane[0:1] < cut_y
        edge = slice(PAD + rows - 1, PAD + rows)
        for c in range(columns):
            for i in range(3):
                north_out[step, i, c : c + 1, :] = field[b, c, i, edge, :]

        @pl.when(has_north)
        def _():
            lat_copy(step, 0).start()

    def send_south(step):
        b = step % 2
        low = lane[0:1] < cut_y
        edge = slice(PAD, PAD + 1)
        for c in range(columns):
            south_out[step, 0, c : c + 1, :] = jnp.where(
                low, field[b, c, 5, edge, :], field[b, c, 2, edge, :]
            )
            for i in range(1, 3):
                south_out[step, i, c : c + 1, :] = field[b, c, i + 2, edge, :]

        @pl.when(has_south)
        def _():
            lat_copy(step, 1).start()

    def take_south(step):
        b = step % 2

        @pl.when(has_south)
        def _():
            lat_copy(step, 0).wait_recv()
            for c in range(columns):
                for i in range(3):
                    field[b, c, i, PAD - 1 : PAD, :] = south_in[step, i, c : c + 1, :]

    def take_north(step):
        b = step % 2
        edge = slice(PAD + rows, PAD + rows + 1)

        @pl.when(has_north)
        def _():
            lat_copy(step, 1).wait_recv()
            for c in range(columns):
                for i, t in ((0, 2), (1, 3), (2, 4), (0, 5)):
                    field[b, c, t, edge, :] = north_in[step, i, c : c + 1, :]

    def advance(step, k, group):
        b = step % 2
        at = slice(PAD + k * piece, PAD + (k + 1) * piece)
        up = slice(at.start - 1, at.stop - 1)
        down = slice(at.start + 1, at.stop + 1)
        span = slice(k * piece, (k + 1) * piece)
        first = group[0]

        def from_west(c, t):
            if c > 0:
                return field[b, c - 1, t, at, :]
            value = west_in[step, {0: 0, 1: 1, 3: 1, 4: 2, 5: 1}[t], span, :]
            return pltpu.roll(value, LANES - SHIFT, 1) if t == 5 else value

        def from_east(c, t):
            if c < columns - 1:
                return field[b, c + 1, t, at, :]
            return east_in[step, t - 1, span, :]

        totals = []
        for n, c in enumerate(group):
            total = None
            for t in range(tiles):
                if t == 1:
                    beside = jnp.where(lane_piece < cut_w, from_west(c, t), from_east(c, t))
                elif t == 2:
                    beside = from_east(c, t)
                elif t == 3:
                    beside = jnp.where(lane_piece < cut_e, from_east(c, t), from_west(c, t))
                else:
                    beside = from_west(c, t)
                if t < 2:
                    along = field[b, c, t, up, :]
                elif t == 2:
                    along = jnp.where(lane_piece < cut_y, field[b, c, t, up, :], field[b, c, t, down, :])
                else:
                    along = field[b, c, t, down, :]
                advected = (
                    keep_x[t, span, :] * field[b, c, t, at, :]
                    + push_x[t, span, :] * beside
                    + push_y[t, 0:1, :] * along
                )
                field[1 - b, c, t, at, :] = advected
                rounded[n * piece : (n + 1) * piece, t * LANES : (t + 1) * LANES] = advected.astype(
                    jnp.bfloat16
                )
                total = advected if total is None else total + advected
            energy = jnp.sum(total, axis=1, keepdims=True) * mean_of
            sea_here = scale[c, span, :]
            totals.append(grow[c, span, :] - (time_step * dissipation) * energy * sea_here)
        size = len(group) * piece
        transfer = jnp.dot(rounded[0:size, :], weights[...], preferred_element_type=jnp.float32)
        for n, c in enumerate(group):
            sea_here = time_step * scale[c, span, :]
            for t in range(tiles):
                moved = transfer[n * piece : (n + 1) * piece, t * LANES : (t + 1) * LANES]
                value = totals[n] * field[1 - b, c, t, at, :] + sea_here * moved
                if step < STEPS - 1:
                    field[1 - b, c, t, at, :] = value
                else:
                    w = width(t)
                    staged[c, span, t * LANES : t * LANES + w] = value[:, 0:w]

    heard = 2 + has_south.astype(jnp.int32) + has_north.astype(jnp.int32)
    pl.semaphore_wait(barrier, heard)

    for n, c in enumerate(order):
        loads[c].wait()
        for t in range(tiles):
            w = width(t)
            field[0, c, t, PAD : PAD + rows, 0:w] = (
                staged[c, :, t * LANES : t * LANES + w] * scale[c, :, 0:w]
            )
        if n == 1:
            for k in range(CHUNKS):
                send_lon(0, k)
    send_north(0)
    send_south(0)

    weight_load.wait()
    weights[...] = jnp.zeros_like(weights)
    weights[0:bins, 0:bins] = raw_weights[...]

    edges, inner = [0, columns - 1], list(range(1, columns - 1))
    stores = []
    for step in range(STEPS):
        for k in range(CHUNKS):
            if k == 0:
                take_south(step)
            if k == CHUNKS - 1:
                take_north(step)
            for side in range(2):
                lon_copy(step, side, k).wait_recv()
            advance(step, k, edges)
            if step < STEPS - 1:
                send_lon(step + 1, k)
            advance(step, k, inner)
            if step < STEPS - 1:
                if k == 0:
                    send_south(step + 1)
                if k == CHUNKS - 1:
                    send_north(step + 1)
            else:
                span = pl.ds(k * piece, piece)
                store = pltpu.make_async_copy(
                    staged.at[:, span, :], out_ref.at[:, span, :], store_sem.at[k]
                )
                store.start()
                stores.append(store)
    for store in stores:
        store.wait()
    for step in range(STEPS):
        for k in range(CHUNKS):
            for side in range(2):
                lon_copy(step, side, k).wait_send()

        @pl.when(has_north)
        def _():
            lat_copy(step, 0).wait_send()

        @pl.when(has_south)
        def _():
            lat_copy(step, 1).wait_send()


def on_device(spectrum, sea_mask, ice_flags, wind_forcing, group_speed, coupling):
    columns, rows, bins = spectrum.shape
    tiles = -(-bins // LANES)
    wide = tiles * LANES
    piece = rows // CHUNKS
    vmem = pl.BlockSpec(memory_space=pltpu.VMEM)
    anywhere = pl.BlockSpec(memory_space=pl.ANY)
    f32 = jnp.float32
    lon_buffer = pltpu.VMEM((STEPS, 3, rows, LANES), f32)
    lat_buffer = pltpu.VMEM((STEPS, 3, columns, LANES), f32)
    return pl.pallas_call(
        functools.partial(kernel, group_speed.shape[0]),
        out_shape=jax.ShapeDtypeStruct(spectrum.shape, spectrum.dtype),
        in_specs=[pl.BlockSpec(memory_space=pltpu.SMEM), vmem, vmem, vmem, anywhere, anywhere],
        out_specs=anywhere,
        scratch_shapes=[
            pltpu.VMEM((2, columns, tiles, rows + 2 * PAD, LANES), f32),
            pltpu.VMEM((columns, rows, bins), f32),
            pltpu.VMEM((wide, wide), jnp.bfloat16),
            pltpu.VMEM((bins, bins), jnp.bfloat16),
            pltpu.VMEM(((columns - 2) * piece, wide), jnp.bfloat16),
            pltpu.VMEM((tiles, rows, LANES), f32),
            pltpu.VMEM((tiles, rows, LANES), f32),
            pltpu.VMEM((tiles, 8, LANES), f32),
            pltpu.VMEM((columns, rows, LANES), f32),
            pltpu.VMEM((columns, rows, LANES), f32),
            lon_buffer, lon_buffer, lon_buffer, lon_buffer,
            lat_buffer, lat_buffer, lat_buffer, lat_buffer,
            pltpu.SemaphoreType.DMA((columns,)),
            pltpu.SemaphoreType.DMA,
            pltpu.SemaphoreType.DMA((CHUNKS,)),
            pltpu.SemaphoreType.DMA((STEPS, 2, CHUNKS)),
            pltpu.SemaphoreType.DMA((STEPS, 2, CHUNKS)),
            pltpu.SemaphoreType.DMA((STEPS, 2)),
            pltpu.SemaphoreType.DMA((STEPS, 2)),
        ],
        compiler_params=pltpu.CompilerParams(
            collective_id=0, has_side_effects=True, vmem_limit_bytes=48 * 1024 * 1024
        ),
    )(group_speed, sea_mask, ice_flags, wind_forcing, spectrum, coupling)


def solution(mesh):
    placed = (P("lon", "lat", None), P("lon", "lat"), P("lon", "lat"), P("lon", "lat"), P(), P())
    return jax.shard_map(
        on_device, mesh=mesh, in_specs=placed, out_specs=P("lon", "lat", None), check_vma=False
    )
```

time: 68.2 us -> 35.5 us (0.52)
  the two profiles are of different devices: /device:TPU:1 before, /device:TPU:0 now
where the time goes in v1:
time: 35.5 us; the launch traced here: 35.2 us
  Pallas kernels  28.8 us (81%)
  local copies, waits for them, and re-layouts  6.47 us (18%)
    pallas_call x1, Pallas kernels, on_device(): pl.pallas_call(functools.partial(kernel, group_speed.shape[0]), out_shape...  28.8 us
    unnamed x13, local copies, waits for them, and re-layouts  6.47 us

profile of v1, /device:TPU:0, one launch (start us, length us, event | category | flops | bytes accessed | tf_op | source)
XLA Modules:
  0.0 35.2 jit_solution(1430601355571872197)
XLA Ops:
  0.0 0.0 copy-start
  0.0 1.4 %copy-done = f32[8,64,648]{2,1,0:T(8,128)S(1)} copy-done((f32[8,64,648]{2,1,0:T(8,128)S(1)}, f32[8,64,648]{2,1,0:T(8,128)}, u32[]{:S(2)}) %copy-start) | copy-done | bytes 1327128
  1.4 0.0 copy-start.1
  1.4 1.2 %copy-done.1 = bf16[648,648]{1,0:T(8,128)(2,1)S(1)} copy-done((bf16[648,648]{1,0:T(8,128)(2,1)S(1)}, bf16[648,648]{1,0:T(8,128)(2,1)}, u32[]{:S(2)}) %copy-start.1) | copy-done | bytes 839832
  2.6 0.0 copy-start.2
  2.6 0.7 %copy-done.2 = s32[8,64]{1,0:T(8,128)S(1)} copy-done((s32[8,64]{1,0:T(8,128)S(1)}, s32[8,64]{1,0:T(8,128)}, u32[]{:S(2)}) %copy-start.2) | copy-done | bytes 2072
  3.3 0.0 copy-start.3
  3.3 0.7 %copy-done.3 = s32[8,64]{1,0:T(8,128)S(1)} copy-done((s32[8,64]{1,0:T(8,128)S(1)}, s32[8,64]{1,0:T(8,128)}, u32[]{:S(2)}) %copy-start.3) | copy-done | bytes 2072
  4.0 0.0 copy-start.4
  4.0 0.7 %copy-done.4 = f32[8,64]{1,0:T(8,128)S(1)} copy-done((f32[8,64]{1,0:T(8,128)S(1)}, f32[8,64]{1,0:T(8,128)}, u32[]{:S(2)}) %copy-start.4) | copy-done | bytes 2072
  4.7 0.0 copy-start.5
  4.7 0.7 %copy-done.5 = f32[18]{0:T(128)S(1)} copy-done((f32[18]{0:T(128)S(1)}, f32[18]{0:T(128)}, u32[]{:S(2)}) %copy-start.5) | copy-done | bytes 96
  5.3 28.8 %shard_map.64 = f32[8,64,648]{2,1,0:T(8,128)S(1)} custom-call(f32[18]{0:T(128)S(1)} %copy-done.5, s32[8,64]{1,0:T(8,128)S(1)} %copy-done.2, s32[8,64]{1,0:T(8,128)S(1)} %copy-done.3, f32[8,64]{1,0:T(8,128)S(1)} %copy-done.4, f32[8,64,648]{2,1,0:T(8,128)S(1)} %copy-done, bf16[648,648]{1,0:T(8,128)(2,1)S(1)} %copy-done.1), custom_call_target="tpu_custom_call" | custom-call | tf_op jit(solution)/shard_map/pallas_call | solution.py:324
  34.1 1.1 %copy.8 = f32[8,64,648]{2,1,0:T(8,128)} copy(f32[8,64,648]{2,1,0:T(8,128)S(1)} %shard_map.64) | data formatting | bytes 2654208
Async XLA Ops:
  0.0 1.4 %copy-start = (f32[8,64,648]{2,1,0:T(8,128)S(1)}, f32[8,64,648]{2,1,0:T(8,128)}, u32[]{:S(2)}) copy-start(f32[8,64,648]{2,1,0:T(8,128)} %spectrum_ref.1) | copy-start | bytes 3981316
  1.4 1.2 %copy-start.1 = (bf16[648,648]{1,0:T(8,128)(2,1)S(1)}, bf16[648,648]{1,0:T(8,128)(2,1)}, u32[]{:S(2)}) copy-start(bf16[648,648]{1,0:T(8,128)(2,1)} %coupling_ref.1) | copy-start | bytes 2519428
  2.6 0.7 %copy-start.2 = (s32[8,64]{1,0:T(8,128)S(1)}, s32[8,64]{1,0:T(8,128)}, u32[]{:S(2)}) copy-start(s32[8,64]{1,0:T(8,128)} %sea_ref.1) | copy-start | bytes 6148
  3.3 0.7 %copy-start.3 = (s32[8,64]{1,0:T(8,128)S(1)}, s32[8,64]{1,0:T(8,128)}, u32[]{:S(2)}) copy-start(s32[8,64]{1,0:T(8,128)} %ice_ref.1) | copy-start | bytes 6148
  4.0 0.7 %copy-start.4 = (f32[8,64]{1,0:T(8,128)S(1)}, f32[8,64]{1,0:T(8,128)}, u32[]{:S(2)}) copy-start(f32[8,64]{1,0:T(8,128)} %wind_ref.1) | copy-start | bytes 6148
  4.7 0.7 %copy-start.5 = (f32[18]{0:T(128)S(1)}, f32[18]{0:T(128)}, u32[]{:S(2)}) copy-start(f32[18]{0:T(128)} %speed_ref.1) | copy-start | bytes 220

commit v2 on v1

--- a/solution.py
+++ b/solution.py
@@ -12,7 +12,7 @@
 STEPS = 4
 LANES = 128
 PAD = 8
-CHUNKS = 2
+CHUNKS = 4
 SHIFT = 40
 MESH = pl.DeviceIdType.MESH
 
@@ -21,10 +21,11 @@
 
 
 def kernel(
-    freqs, speed_ref, sea_ref, ice_ref, wind_ref, spectrum_ref, coupling_ref, out_ref,
+    freqs, speed_hbm, sea_hbm, ice_hbm, wind_hbm, spectrum_ref, coupling_ref, out_ref,
+    speed_ref, sea_ref, ice_ref, wind_ref,
     field, staged, weights, raw_weights, rounded, keep_x, push_x, push_y, grow, scale,
     east_out, east_in, west_out, west_in, north_out, north_in, south_out, south_in,
-    load_sem, weight_sem, store_sem, lon_send, lon_recv, lat_send, lat_recv,
+    load_sem, small_sem, weight_sem, store_sem, lon_send, lon_recv, lat_send, lat_recv,
 ):
     columns, rows, bins = staged.shape
     tiles = field.shape[2]
@@ -46,6 +47,14 @@
     loads = {
         c: pltpu.make_async_copy(spectrum_ref.at[c], staged.at[c], load_sem.at[c]) for c in order
     }
+    small = [
+        pltpu.make_async_copy(source, target, small_sem.at[n])
+        for n, (source, target) in enumerate(
+            ((speed_hbm, speed_ref), (sea_hbm, sea_ref), (ice_hbm, ice_ref), (wind_hbm, wind_ref))
+        )
+    ]
+    for copy in small:
+        copy.start()
     for c in order:
         loads[c].start()
     weight_load = pltpu.make_async_copy(coupling_ref, raw_weights, weight_sem)
@@ -63,6 +72,8 @@
     def _():
         pl.semaphore_signal(barrier, inc=1, device_id=(lon, lat + 1), device_id_type=MESH)
 
+    for copy in small:
+        copy.wait()
     sea = sea_ref[...].astype(jnp.float32)
     forcing = wind_ref[...] * (1.0 - ice_ref[...].astype(jnp.float32))
     growth = jnp.transpose(sea * (1.0 + time_step * forcing))
@@ -316,7 +327,7 @@
     tiles = -(-bins // LANES)
     wide = tiles * LANES
     piece = rows // CHUNKS
-    vmem = pl.BlockSpec(memory_space=pltpu.VMEM)
+    hbm = pl.BlockSpec(memory_space=pltpu.HBM)
     anywhere = pl.BlockSpec(memory_space=pl.ANY)
     f32 = jnp.float32
     lon_buffer = pltpu.VMEM((STEPS, 3, rows, LANES), f32)
@@ -324,9 +335,13 @@
     return pl.pallas_call(
         functools.partial(kernel, group_speed.shape[0]),
         out_shape=jax.ShapeDtypeStruct(spectrum.shape, spectrum.dtype),
-        in_specs=[pl.BlockSpec(memory_space=pltpu.SMEM), vmem, vmem, vmem, anywhere, anywhere],
+        in_specs=[hbm] * 6,
         out_specs=anywhere,
         scratch_shapes=[
+            pltpu.SMEM(group_speed.shape, f32),
+            pltpu.VMEM((columns, rows), jnp.int32),
+            pltpu.VMEM((columns, rows), jnp.int32),
+            pltpu.VMEM((columns, rows), f32),
             pltpu.VMEM((2, columns, tiles, rows + 2 * PAD, LANES), f32),
             pltpu.VMEM((columns, rows, bins), f32),
             pltpu.VMEM((wide, wide), jnp.bfloat16),
@@ -340,6 +355,7 @@
             lon_buffer, lon_buffer, lon_buffer, lon_buffer,
             lat_buffer, lat_buffer, lat_buffer, lat_buffer,
             pltpu.SemaphoreType.DMA((columns,)),
+            pltpu.SemaphoreType.DMA((4,)),
             pltpu.SemaphoreType.DMA,
             pltpu.SemaphoreType.DMA((CHUNKS,)),
             pltpu.SemaphoreType.DMA((STEPS, 2, CHUNKS)),
@@ -348,7 +364,7 @@
             pltpu.SemaphoreType.DMA((STEPS, 2)),
         ],
         compiler_params=pltpu.CompilerParams(
-            collective_id=0, has_side_effects=True, vmem_limit_bytes=48 * 1024 * 1024
+            collective_id=0, has_side_effects=True, vmem_limit_bytes=60 * 1024 * 1024
         ),
     )(group_speed, sea_mask, ice_flags, wind_forcing, spectrum, coupling)
 

time: 35.5 us -> 28.8 us (0.81)
  local copies, waits for them, and re-layouts: 6.47 us -> 2.67 us
  Pallas kernels: 28.8 us -> 25.9 us
    unnamed x13 -> x1, local copies, waits for them, and re-layouts: 6.47 us -> 2.67 us
    pallas_call x1, Pallas kernels: 28.8 us -> 25.9 us  [on_device(): pl.pallas_call(functools.partial(kernel, group_speed.shape[0]), out_shape...]
where the time goes in v2:
time: 28.8 us; the launch traced here: 28.6 us
  Pallas kernels  25.9 us (90%)
  local copies, waits for them, and re-layouts  2.67 us (9%)
    pallas_call x1, Pallas kernels, on_device(): pl.pallas_call(functools.partial(kernel, group_speed.shape[0]), out_shape...  25.9 us
    unnamed x1, local copies, waits for them, and re-layouts  2.67 us

profile of v2, /device:TPU:0, one launch (start us, length us, event | category | flops | bytes accessed | tf_op | source)
XLA Modules:
  0.0 28.6 jit_solution(6527118967139196828)
XLA Ops:
  0.0 25.9 %shard_map.64 = f32[8,64,648]{2,1,0:T(8,128)} custom-call(f32[18]{0:T(128)} %speed_hbm.1, s32[8,64]{1,0:T(8,128)} %sea_hbm.1, s32[8,64]{1,0:T(8,128)} %ice_hbm.1, f32[8,64]{1,0:T(8,128)} %wind_hbm.1, f32[8,64,648]{2,1,0:T(8,128)} %spectrum_ref.1, bf16[648,648]{1,0:T(8,128)(2,1)} %coupling_ref.1), custom_call_target="tpu_custom_call" | custom-call | tf_op jit(solution)/shard_map/pallas_call | solution.py:335
  25.9 2.7 %copy.8 = f32[8,64,648]{2,1,0:T(8,128)} copy(f32[8,64,648]{2,1,0:T(8,128)} %shard_map.64) | data formatting | bytes 2654208

commit v3 on v2

--- a/solution.py
+++ b/solution.py
@@ -13,7 +13,6 @@
 LANES = 128
 PAD = 8
 CHUNKS = 4
-SHIFT = 40
 MESH = pl.DeviceIdType.MESH
 
 time_step = 0.2
@@ -25,7 +24,7 @@
     speed_ref, sea_ref, ice_ref, wind_ref,
     field, staged, weights, raw_weights, rounded, keep_x, push_x, push_y, grow, scale,
     east_out, east_in, west_out, west_in, north_out, north_in, south_out, south_in,
-    load_sem, small_sem, weight_sem, store_sem, lon_send, lon_recv, lat_send, lat_recv,
+    load_sem, small_sem, weight_sem, lon_send, lon_recv, lat_send, lat_recv,
 ):
     columns, rows, bins = staged.shape
     tiles = field.shape[2]
@@ -33,6 +32,7 @@
     mean_of = 1.0 / bins
     quarter, half, late = DIRS // 4 * freqs, DIRS // 2 * freqs, DIRS * 3 // 4 * freqs
     cut_w, cut_y, cut_e = quarter - LANES, half - 2 * LANES, late - 3 * LANES
+    late_w = LANES - cut_e
     tail = bins - (tiles - 1) * LANES
 
     lon, lat = lax.axis_index("lon"), lax.axis_index("lat")
@@ -43,22 +43,23 @@
     def width(t):
         return LANES if t < tiles - 1 else tail
 
-    order = [0, columns - 1] + list(range(1, columns - 1))
-    loads = {
-        c: pltpu.make_async_copy(spectrum_ref.at[c], staged.at[c], load_sem.at[c]) for c in order
-    }
+    last = columns - 1
+    edges, inner = [0, last], list(range(1, last))
+    loads = [
+        pltpu.make_async_copy(spectrum_ref.at[c], staged.at[c], load_sem.at[c])
+        for c in range(columns)
+    ]
+    weight_load = pltpu.make_async_copy(coupling_ref, raw_weights, weight_sem)
     small = [
         pltpu.make_async_copy(source, target, small_sem.at[n])
         for n, (source, target) in enumerate(
-            ((speed_hbm, speed_ref), (sea_hbm, sea_ref), (ice_hbm, ice_ref), (wind_hbm, wind_ref))
+            ((sea_hbm, sea_ref), (speed_hbm, speed_ref), (ice_hbm, ice_ref), (wind_hbm, wind_ref))
         )
     ]
     for copy in small:
         copy.start()
-    for c in order:
+    for c in edges:
         loads[c].start()
-    weight_load = pltpu.make_async_copy(coupling_ref, raw_weights, weight_sem)
-    weight_load.start()
 
     barrier = pltpu.get_barrier_semaphore()
     pl.semaphore_signal(barrier, inc=1, device_id=(east, lat), device_id_type=MESH)
@@ -72,51 +73,43 @@
     def _():
         pl.semaphore_signal(barrier, inc=1, device_id=(lon, lat + 1), device_id_type=MESH)
 
-    for copy in small:
-        copy.wait()
+    small[0].wait()
     sea = sea_ref[...].astype(jnp.float32)
-    forcing = wind_ref[...] * (1.0 - ice_ref[...].astype(jnp.float32))
-    growth = jnp.transpose(sea * (1.0 + time_step * forcing))
     sea_rows = jnp.transpose(sea)
     for c in range(columns):
-        grow[c] = jnp.broadcast_to(growth[:, c : c + 1], (rows, LANES))
         scale[c] = jnp.broadcast_to(sea_rows[:, c : c + 1], (rows, LANES))
 
     lane = lax.broadcasted_iota(jnp.int32, (8, LANES), 1)
     lane_piece = lax.broadcasted_iota(jnp.int32, (piece, LANES), 1)
-    row = lax.broadcasted_iota(jnp.int32, (rows, LANES), 0) + lat * rows
-    latitude = (-60.0 + 120.0 * (row.astype(jnp.float32) + 0.5) / (rows * lats)) * (math.pi / 180.0)
-    inverse = 1.0 / jnp.cos(latitude)
-    for t in range(tiles):
-        number = (lane + t * LANES).astype(jnp.float32)
-        direction = jnp.floor((number + 0.5) * (1.0 / freqs))
-        freq = number - direction * freqs
-        speed = jnp.zeros((8, LANES), jnp.float32)
-        for f in range(freqs):
-            speed = jnp.where(freq == f, speed_ref[f], speed)
-        inside = (lane + t * LANES) < bins
-        theta = (direction + 0.5) * (2.0 * math.pi / DIRS)
-        along_y = jnp.where(inside, jnp.abs(0.45 * jnp.sin(theta) * speed), 0.0)
-        along_x = jnp.where(inside, jnp.abs(0.225 * jnp.cos(theta) * speed), 0.0)
-        push_y[t] = along_y
-        along_x = along_x[0:1] * inverse
-        push_x[t] = along_x
-        keep_x[t] = 1.0 - along_x - along_y[0:1]
-
-    zero_row = jnp.zeros((1, LANES), jnp.float32)
-    for c in range(columns):
-        for t in range(tiles):
-            for b in range(2):
-                field[b, c, t, PAD - 1 : PAD, :] = zero_row
-                field[b, c, t, PAD + rows : PAD + rows + 1, :] = zero_row
-        field[0, c, tiles - 1, PAD : PAD + rows, :] = jnp.zeros((rows, LANES), jnp.float32)
+    lane_eight = lax.broadcasted_iota(jnp.int32, (8, LANES), 1)
+    row_eight = lax.broadcasted_iota(jnp.int32, (8, LANES), 0)
+    own_low = lane_eight // 4 == row_eight
+    own_high = lane_eight // 4 == row_eight + 8
+    low_half = lane_eight < LANES // 2
+
+    def pack(buffer, loose):
+        upper, lower = loose[0:8], loose[8:16]
+        buffer[32:40, :] = jnp.where(low_half, upper, pltpu.roll(lower, 64, 1))
+        spread = jnp.where(own_low, pltpu.roll(upper, 64, 1, stride=4, stride_axis=0), 0.0)
+        spread += jnp.where(own_high, pltpu.roll(lower, 96, 1, stride=4, stride_axis=0), 0.0)
+        buffer[40:41, :] = jnp.sum(spread, axis=0, keepdims=True)
+
+    def unpack(buffer):
+        main = buffer[32:40, :]
+        rest = jnp.broadcast_to(buffer[40:41, :], (8, LANES))
+        rest = pltpu.roll(rest, 64, 1)
+        for bit in range(3):
+            moved = pltpu.roll(rest, LANES - 4 * 2**bit, 1)
+            rest = jnp.where(row_eight // 2**bit % 2 == 1, moved, rest)
+        upper = jnp.where(low_half, main, rest)
+        lower = jnp.where(low_half, pltpu.roll(main, 64, 1), pltpu.roll(rest, 96, 1))
+        return jnp.concatenate([upper, lower], axis=0)
 
     def lon_copy(step, side, k):
-        span = pl.ds(k * piece, piece)
         out_buf, in_buf, to = ((east_out, west_in, east), (west_out, east_in, west))[side]
         return pltpu.make_async_remote_copy(
-            src_ref=out_buf.at[step, :, span, :],
-            dst_ref=in_buf.at[step, :, span, :],
+            src_ref=out_buf.at[step, k],
+            dst_ref=in_buf.at[step, k],
             send_sem=lon_send.at[step, side, k],
             recv_sem=lon_recv.at[step, side, k],
             device_id=(to, lat),
@@ -136,16 +129,24 @@
 
     def send_lon(step, k):
         b = step % 2
-        span = slice(k * piece, (k + 1) * piece)
         at = slice(PAD + k * piece, PAD + (k + 1) * piece)
-        last = columns - 1
-        east_out[step, 0, span, :] = field[b, last, 0, at, :]
-        end = pltpu.roll(field[b, last, 5, at, :], SHIFT, 1)
-        mixed = jnp.where(lane_piece < cut_w, field[b, last, 1, at, :], end)
-        east_out[step, 1, span, :] = jnp.where(lane_piece < cut_e, mixed, field[b, last, 3, at, :])
-        east_out[step, 2, span, :] = field[b, last, 4, at, :]
-        for i in range(3):
-            west_out[step, i, span, :] = field[b, 0, i + 1, at, :]
+        buffer = east_out.at[step, k]
+        buffer[0:16, :] = field[b, last, 0, at, :]
+        buffer[16:32, :] = field[b, last, 4, at, :]
+        loose = jnp.where(
+            lane_piece < cut_w + late_w,
+            pltpu.roll(field[b, last, 1, at, :], late_w, 1),
+            pltpu.roll(field[b, last, 5, at, :], cut_w + late_w, 1),
+        )
+        pack(
+            buffer,
+            jnp.where(lane_piece < late_w, pltpu.roll(field[b, last, 3, at, :], late_w, 1), loose),
+        )
+        buffer = west_out.at[step, k]
+        first_part = field[b, 0, 1, at, :]
+        buffer[0:16, :] = field[b, 0, 2, at, :]
+        buffer[16:32, :] = jnp.where(lane_piece < cut_e, field[b, 0, 3, at, :], first_part)
+        pack(buffer, pltpu.roll(first_part, LANES - cut_w, 1))
         lon_copy(step, 0, k).start()
         lon_copy(step, 1, k).start()
 
@@ -203,18 +204,30 @@
         up = slice(at.start - 1, at.stop - 1)
         down = slice(at.start + 1, at.stop + 1)
         span = slice(k * piece, (k + 1) * piece)
-        first = group[0]
+        if 0 in group:
+            buffer = west_in.at[step, k]
+            loose = unpack(buffer)
+            shared = pltpu.roll(loose, LANES - late_w, 1)
+            west_halo = {
+                0: buffer[0:16, :],
+                1: shared,
+                3: shared,
+                4: buffer[16:32, :],
+                5: pltpu.roll(loose, LANES - cut_w - late_w, 1),
+            }
+        if last in group:
+            buffer = east_in.at[step, k]
+            shared = buffer[16:32, :]
+            moved = pltpu.roll(unpack(buffer), cut_w, 1)
+            east_halo = {
+                1: jnp.where(lane_piece < cut_e, moved, shared), 2: buffer[0:16, :], 3: shared
+            }
 
         def from_west(c, t):
-            if c > 0:
-                return field[b, c - 1, t, at, :]
-            value = west_in[step, {0: 0, 1: 1, 3: 1, 4: 2, 5: 1}[t], span, :]
-            return pltpu.roll(value, LANES - SHIFT, 1) if t == 5 else value
+            return field[b, c - 1, t, at, :] if c > 0 else west_halo[t]
 
         def from_east(c, t):
-            if c < columns - 1:
-                return field[b, c + 1, t, at, :]
-            return east_in[step, t - 1, span, :]
+            return field[b, c + 1, t, at, :] if c < last else east_halo[t]
 
         totals = []
         for n, c in enumerate(group):
@@ -258,21 +271,67 @@
                     field[1 - b, c, t, at, :] = value
                 else:
                     w = width(t)
-                    staged[c, span, t * LANES : t * LANES + w] = value[:, 0:w]
+                    out_ref[c, span, t * LANES : t * LANES + w] = value[:, 0:w]
 
     heard = 2 + has_south.astype(jnp.int32) + has_north.astype(jnp.int32)
     pl.semaphore_wait(barrier, heard)
 
-    for n, c in enumerate(order):
-        loads[c].wait()
+    def take_column(c):
         for t in range(tiles):
             w = width(t)
             field[0, c, t, PAD : PAD + rows, 0:w] = (
                 staged[c, :, t * LANES : t * LANES + w] * scale[c, :, 0:w]
             )
-        if n == 1:
-            for k in range(CHUNKS):
-                send_lon(0, k)
+
+    for c in edges:
+        field[0, c, tiles - 1, PAD : PAD + rows, :] = jnp.zeros((rows, LANES), jnp.float32)
+    for c in edges:
+        loads[c].wait()
+    for c in inner:
+        loads[c].start()
+    weight_load.start()
+    for c in edges:
+        take_column(c)
+    for k in range(CHUNKS):
+        send_lon(0, k)
+
+    for copy in small[1:]:
+        copy.wait()
+    forcing = wind_ref[...] * (1.0 - ice_ref[...].astype(jnp.float32))
+    growth = jnp.transpose(sea * (1.0 + time_step * forcing))
+    for c in range(columns):
+        grow[c] = jnp.broadcast_to(growth[:, c : c + 1], (rows, LANES))
+    row = lax.broadcasted_iota(jnp.int32, (rows, LANES), 0) + lat * rows
+    latitude = (-60.0 + 120.0 * (row.astype(jnp.float32) + 0.5) / (rows * lats)) * (math.pi / 180.0)
+    inverse = 1.0 / jnp.cos(latitude)
+    for t in range(tiles):
+        number = (lane + t * LANES).astype(jnp.float32)
+        direction = jnp.floor((number + 0.5) * (1.0 / freqs))
+        freq = number - direction * freqs
+        speed = jnp.zeros((8, LANES), jnp.float32)
+        for f in range(freqs):
+            speed = jnp.where(freq == f, speed_ref[f], speed)
+        inside = (lane + t * LANES) < bins
+        theta = (direction + 0.5) * (2.0 * math.pi / DIRS)
+        along_y = jnp.where(inside, jnp.abs(0.45 * jnp.sin(theta) * speed), 0.0)
+        along_x = jnp.where(inside, jnp.abs(0.225 * jnp.cos(theta) * speed), 0.0)
+        push_y[t] = along_y
+        along_x = along_x[0:1] * inverse
+        push_x[t] = along_x
+        keep_x[t] = 1.0 - along_x - along_y[0:1]
+
+    zero_row = jnp.zeros((1, LANES), jnp.float32)
+    for c in range(columns):
+        for t in range(tiles):
+            for b in range(2):
+                field[b, c, t, PAD - 1 : PAD, :] = zero_row
+                field[b, c, t, PAD + rows : PAD + rows + 1, :] = zero_row
+        if c in inner:
+            field[0, c, tiles - 1, PAD : PAD + rows, :] = jnp.zeros((rows, LANES), jnp.float32)
+
+    for c in inner:
+        loads[c].wait()
+        take_column(c)
     send_north(0)
     send_south(0)
 
@@ -280,9 +339,7 @@
     weights[...] = jnp.zeros_like(weights)
     weights[0:bins, 0:bins] = raw_weights[...]
 
-    edges, inner = [0, columns - 1], list(range(1, columns - 1))
-    stores = []
-    for step in range(STEPS):
+    for step in range(STEPS - 1):
         for k in range(CHUNKS):
             if k == 0:
                 take_south(step)
@@ -291,23 +348,20 @@
             for side in range(2):
                 lon_copy(step, side, k).wait_recv()
             advance(step, k, edges)
-            if step < STEPS - 1:
-                send_lon(step + 1, k)
+            send_lon(step + 1, k)
             advance(step, k, inner)
-            if step < STEPS - 1:
-                if k == 0:
-                    send_south(step + 1)
-                if k == CHUNKS - 1:
-                    send_north(step + 1)
-            else:
-                span = pl.ds(k * piece, piece)
-                store = pltpu.make_async_copy(
-                    staged.at[:, span, :], out_ref.at[:, span, :], store_sem.at[k]
-                )
-                store.start()
-                stores.append(store)
-    for store in stores:
-        store.wait()
+            if k == 0:
+                send_south(step + 1)
+            if k == CHUNKS - 1:
+                send_north(step + 1)
+    take_south(STEPS - 1)
+    take_north(STEPS - 1)
+    for k in range(CHUNKS):
+        advance(STEPS - 1, k, inner)
+    for k in range(CHUNKS):
+        for side in range(2):
+            lon_copy(STEPS - 1, side, k).wait_recv()
+        advance(STEPS - 1, k, edges)
     for step in range(STEPS):
         for k in range(CHUNKS):
             for side in range(2):
@@ -328,15 +382,15 @@
     wide = tiles * LANES
     piece = rows // CHUNKS
     hbm = pl.BlockSpec(memory_space=pltpu.HBM)
-    anywhere = pl.BlockSpec(memory_space=pl.ANY)
+    operands = (group_speed, sea_mask, ice_flags, wind_forcing, spectrum, coupling)
     f32 = jnp.float32
-    lon_buffer = pltpu.VMEM((STEPS, 3, rows, LANES), f32)
+    lon_buffer = pltpu.VMEM((STEPS, CHUNKS, 41, LANES), f32)
     lat_buffer = pltpu.VMEM((STEPS, 3, columns, LANES), f32)
     return pl.pallas_call(
         functools.partial(kernel, group_speed.shape[0]),
         out_shape=jax.ShapeDtypeStruct(spectrum.shape, spectrum.dtype),
         in_specs=[hbm] * 6,
-        out_specs=anywhere,
+        out_specs=pl.BlockSpec(memory_space=pltpu.VMEM),
         scratch_shapes=[
             pltpu.SMEM(group_speed.shape, f32),
             pltpu.VMEM((columns, rows), jnp.int32),
@@ -357,16 +411,15 @@
             pltpu.SemaphoreType.DMA((columns,)),
             pltpu.SemaphoreType.DMA((4,)),
             pltpu.SemaphoreType.DMA,
-            pltpu.SemaphoreType.DMA((CHUNKS,)),
             pltpu.SemaphoreType.DMA((STEPS, 2, CHUNKS)),
             pltpu.SemaphoreType.DMA((STEPS, 2, CHUNKS)),
             pltpu.SemaphoreType.DMA((STEPS, 2)),
             pltpu.SemaphoreType.DMA((STEPS, 2)),
         ],
         compiler_params=pltpu.CompilerParams(
-            collective_id=0, has_side_effects=True, vmem_limit_bytes=60 * 1024 * 1024
+            collective_id=0, has_side_effects=True, vmem_limit_bytes=32 * 1024 * 1024
         ),
-    )(group_speed, sea_mask, ice_flags, wind_forcing, spectrum, coupling)
+    )(*(pltpu.with_memory_space_constraint(x, pltpu.HBM) for x in operands))
 
 
 def solution(mesh):

time: 28.8 us -> 31.4 us (1.090)
  the two profiles are of different devices: /device:TPU:0 before, /device:TPU:24 now
where the time goes in v3:
time: 31.4 us; the launch traced here: 31.2 us
  Pallas kernels  30.1 us (96%)
  local copies, waits for them, and re-layouts  1.15 us (4%)
    pallas_call x1, Pallas kernels, on_device(): pl.pallas_call(functools.partial(kernel, group_speed.shape[0]), out_shape...  30.1 us
    unnamed x1, local copies, waits for them, and re-layouts  1.15 us

profile of v3, /device:TPU:24, one launch (start us, length us, event | category | flops | bytes accessed | tf_op | source)
XLA Modules:
  0.0 31.2 jit_solution(4666931183111299108)
XLA Ops:
  0.0 30.1 %shard_map.64 = f32[8,64,648]{2,1,0:T(8,128)S(1)} custom-call(f32[18]{0:T(128)} %speed_hbm.1, s32[8,64]{1,0:T(8,128)} %sea_hbm.1, s32[8,64]{1,0:T(8,128)} %ice_hbm.1, f32[8,64]{1,0:T(8,128)} %wind_hbm.1, f32[8,64,648]{2,1,0:T(8,128)} %spectrum_ref.1, bf16[648,648]{1,0:T(8,128)(2,1)} %coupling_ref.1), custom_call_target="tpu_custom_call" | custom-call | tf_op jit(solution)/shard_map/pallas_call | solution.py:389
  30.1 1.1 %copy.8 = f32[8,64,648]{2,1,0:T(8,128)} copy(f32[8,64,648]{2,1,0:T(8,128)S(1)} %shard_map.64) | data formatting | bytes 2654208

commit v4 on v3

--- a/solution.py
+++ b/solution.py
@@ -83,27 +83,29 @@
     lane_piece = lax.broadcasted_iota(jnp.int32, (piece, LANES), 1)
     lane_eight = lax.broadcasted_iota(jnp.int32, (8, LANES), 1)
     row_eight = lax.broadcasted_iota(jnp.int32, (8, LANES), 0)
-    own_low = lane_eight // 4 == row_eight
-    own_high = lane_eight // 4 == row_eight + 8
+    own_low = lane_eight // 4 == row_eight + 1
+    own_high = lane_eight // 4 == row_eight + 9
     low_half = lane_eight < LANES // 2
 
-    def pack(buffer, loose):
-        upper, lower = loose[0:8], loose[8:16]
-        buffer[32:40, :] = jnp.where(low_half, upper, pltpu.roll(lower, 64, 1))
-        spread = jnp.where(own_low, pltpu.roll(upper, 64, 1, stride=4, stride_axis=0), 0.0)
-        spread += jnp.where(own_high, pltpu.roll(lower, 96, 1, stride=4, stride_axis=0), 0.0)
-        buffer[40:41, :] = jnp.sum(spread, axis=0, keepdims=True)
-
-    def unpack(buffer):
-        main = buffer[32:40, :]
-        rest = jnp.broadcast_to(buffer[40:41, :], (8, LANES))
-        rest = pltpu.roll(rest, 64, 1)
-        for bit in range(3):
-            moved = pltpu.roll(rest, LANES - 4 * 2**bit, 1)
-            rest = jnp.where(row_eight // 2**bit % 2 == 1, moved, rest)
-        upper = jnp.where(low_half, main, rest)
-        lower = jnp.where(low_half, pltpu.roll(main, 64, 1), pltpu.roll(rest, 96, 1))
-        return jnp.concatenate([upper, lower], axis=0)
+    def turn(value, by):
+        return pltpu.roll(value, by % LANES, 1)
+
+    def gather_rest(upper, lower, start):
+        base = (4 - start) % LANES
+        up = pltpu.roll(upper, base, 1, stride=4, stride_axis=0)
+        down = pltpu.roll(lower, base + 32, 1, stride=4, stride_axis=0)
+        spread = jnp.where(own_low, up, 0.0) + jnp.where(own_high, down, 0.0)
+        return jnp.sum(spread, axis=0, keepdims=True)
+
+    def spread_rest(line, start):
+        line = jnp.broadcast_to(line, (8, LANES))
+        halves = []
+        for part in range(2):
+            value = turn(line, start - 4 - 32 * part)
+            for i in range(1, 8):
+                value = jnp.where(row_eight == i, turn(line, start - 4 - 4 * i - 32 * part), value)
+            halves.append(value)
+        return halves
 
     def lon_copy(step, side, k):
         out_buf, in_buf, to = ((east_out, west_in, east), (west_out, east_in, west))[side]
@@ -133,20 +135,31 @@
         buffer = east_out.at[step, k]
         buffer[0:16, :] = field[b, last, 0, at, :]
         buffer[16:32, :] = field[b, last, 4, at, :]
-        loose = jnp.where(
-            lane_piece < cut_w + late_w,
-            pltpu.roll(field[b, last, 1, at, :], late_w, 1),
-            pltpu.roll(field[b, last, 5, at, :], cut_w + late_w, 1),
-        )
-        pack(
-            buffer,
-            jnp.where(lane_piece < late_w, pltpu.roll(field[b, last, 3, at, :], late_w, 1), loose),
+        ends = []
+        for part in range(2):
+            rows_at = slice(at.start + 8 * part, at.start + 8 * part + 8)
+            move, offset = late_w + 64 * part, lane_eight - 64 * part
+            value = jnp.where(
+                offset < cut_w + late_w,
+                turn(field[b, last, 1, rows_at, :], move),
+                turn(field[b, last, 5, rows_at, :], move + cut_w),
+            )
+            ends.append(
+                jnp.where(offset < late_w, turn(field[b, last, 3, rows_at, :], move), value)
+            )
+        buffer[32:40, :] = jnp.where(low_half, ends[0], ends[1])
+        buffer[40:41, :] = gather_rest(
+            field[b, last, 5, at.start : at.start + 8, :], field[b, last, 5, at.start + 8 : at.stop, :],
+            64 - late_w - cut_w,
         )
         buffer = west_out.at[step, k]
         first_part = field[b, 0, 1, at, :]
         buffer[0:16, :] = field[b, 0, 2, at, :]
         buffer[16:32, :] = jnp.where(lane_piece < cut_e, field[b, 0, 3, at, :], first_part)
-        pack(buffer, pltpu.roll(first_part, LANES - cut_w, 1))
+        buffer[32:40, :] = jnp.where(
+            low_half, turn(first_part[0:8], -cut_w), turn(first_part[8:16], 64 - cut_w)
+        )
+        buffer[40:41, :] = gather_rest(first_part[0:8], first_part[8:16], 64 + cut_w)
         lon_copy(step, 0, k).start()
         lon_copy(step, 1, k).start()
 
@@ -206,19 +219,29 @@
         span = slice(k * piece, (k + 1) * piece)
         if 0 in group:
             buffer = west_in.at[step, k]
-            loose = unpack(buffer)
-            shared = pltpu.roll(loose, LANES - late_w, 1)
+            main, inside = buffer[32:40, :], 64 - late_w - cut_w
+            rest = spread_rest(buffer[40:41, :], inside)
+            shared = jnp.concatenate([turn(main, -late_w), turn(main, 64 - late_w)], axis=0)
+            ends = [
+                jnp.where(lane_eight < inside, turn(main, 64 * part + inside - 64), rest[part])
+                for part in range(2)
+            ]
             west_halo = {
                 0: buffer[0:16, :],
                 1: shared,
                 3: shared,
                 4: buffer[16:32, :],
-                5: pltpu.roll(loose, LANES - cut_w - late_w, 1),
+                5: jnp.concatenate(ends, axis=0),
             }
         if last in group:
             buffer = east_in.at[step, k]
-            shared = buffer[16:32, :]
-            moved = pltpu.roll(unpack(buffer), cut_w, 1)
+            main, shared = buffer[32:40, :], buffer[16:32, :]
+            rest = spread_rest(buffer[40:41, :], 64 + cut_w)
+            moved = [
+                jnp.where(lane_eight < 64 + cut_w, turn(main, cut_w - 64 * part), rest[part])
+                for part in range(2)
+            ]
+            moved = jnp.concatenate(moved, axis=0)
             east_halo = {
                 1: jnp.where(lane_piece < cut_e, moved, shared), 2: buffer[0:16, :], 3: shared
             }

time: 31.4 us -> 25.3 us (0.81)
  the two profiles are of different devices: /device:TPU:24 before, /device:TPU:0 now
where the time goes in v4:
time: 25.3 us; the launch traced here: 24.9 us
  Pallas kernels  23.8 us (94%)
  local copies, waits for them, and re-layouts  1.15 us (5%)
    pallas_call x1, Pallas kernels, on_device(): pl.pallas_call(functools.partial(kernel, group_speed.shape[0]), out_shape...  23.8 us
    unnamed x1, local copies, waits for them, and re-layouts  1.15 us

profile of v4, /device:TPU:0, one launch (start us, length us, event | category | flops | bytes accessed | tf_op | source)
XLA Modules:
  0.0 24.9 jit_solution(7636494641651076637)
XLA Ops:
  0.0 23.8 %shard_map.64 = f32[8,64,648]{2,1,0:T(8,128)S(1)} custom-call(f32[18]{0:T(128)} %speed_hbm.1, s32[8,64]{1,0:T(8,128)} %sea_hbm.1, s32[8,64]{1,0:T(8,128)} %ice_hbm.1, f32[8,64]{1,0:T(8,128)} %wind_hbm.1, f32[8,64,648]{2,1,0:T(8,128)} %spectrum_ref.1, bf16[648,648]{1,0:T(8,128)(2,1)} %coupling_ref.1), custom_call_target="tpu_custom_call" | custom-call | tf_op jit(solution)/shard_map/pallas_call | solution.py:412
  23.8 1.1 %copy.8 = f32[8,64,648]{2,1,0:T(8,128)} copy(f32[8,64,648]{2,1,0:T(8,128)S(1)} %shard_map.64) | data formatting | bytes 2654208

commit v5 on v4

--- a/solution.py
+++ b/solution.py
@@ -211,12 +211,14 @@
                 for i, t in ((0, 2), (1, 3), (2, 4), (0, 5)):
                     field[b, c, t, edge, :] = north_in[step, i, c : c + 1, :]
 
-    def advance(step, k, group):
-        b = step % 2
-        at = slice(PAD + k * piece, PAD + (k + 1) * piece)
+    def advance(step, k, group, count=1):
+        deep = count * piece
+        lane_deep = lax.broadcasted_iota(jnp.int32, (deep, LANES), 1)
+        b = step % 2
+        at = slice(PAD + k * piece, PAD + (k + count) * piece)
         up = slice(at.start - 1, at.stop - 1)
         down = slice(at.start + 1, at.stop + 1)
-        span = slice(k * piece, (k + 1) * piece)
+        span = slice(k * piece, (k + count) * piece)
         if 0 in group:
             buffer = west_in.at[step, k]
             main, inside = buffer[32:40, :], 64 - late_w - cut_w
@@ -243,7 +245,7 @@
             ]
             moved = jnp.concatenate(moved, axis=0)
             east_halo = {
-                1: jnp.where(lane_piece < cut_e, moved, shared), 2: buffer[0:16, :], 3: shared
+                1: jnp.where(lane_deep < cut_e, moved, shared), 2: buffer[0:16, :], 3: shared
             }
 
         def from_west(c, t):
@@ -257,17 +259,17 @@
             total = None
             for t in range(tiles):
                 if t == 1:
-                    beside = jnp.where(lane_piece < cut_w, from_west(c, t), from_east(c, t))
+                    beside = jnp.where(lane_deep < cut_w, from_west(c, t), from_east(c, t))
                 elif t == 2:
                     beside = from_east(c, t)
                 elif t == 3:
-                    beside = jnp.where(lane_piece < cut_e, from_east(c, t), from_west(c, t))
+                    beside = jnp.where(lane_deep < cut_e, from_east(c, t), from_west(c, t))
                 else:
                     beside = from_west(c, t)
                 if t < 2:
                     along = field[b, c, t, up, :]
                 elif t == 2:
-                    along = jnp.where(lane_piece < cut_y, field[b, c, t, up, :], field[b, c, t, down, :])
+                    along = jnp.where(lane_deep < cut_y, field[b, c, t, up, :], field[b, c, t, down, :])
                 else:
                     along = field[b, c, t, down, :]
                 advected = (
@@ -276,19 +278,19 @@
                     + push_y[t, 0:1, :] * along
                 )
                 field[1 - b, c, t, at, :] = advected
-                rounded[n * piece : (n + 1) * piece, t * LANES : (t + 1) * LANES] = advected.astype(
+                rounded[n * deep : (n + 1) * deep, t * LANES : (t + 1) * LANES] = advected.astype(
                     jnp.bfloat16
                 )
                 total = advected if total is None else total + advected
             energy = jnp.sum(total, axis=1, keepdims=True) * mean_of
             sea_here = scale[c, span, :]
             totals.append(grow[c, span, :] - (time_step * dissipation) * energy * sea_here)
-        size = len(group) * piece
+        size = len(group) * deep
         transfer = jnp.dot(rounded[0:size, :], weights[...], preferred_element_type=jnp.float32)
         for n, c in enumerate(group):
             sea_here = time_step * scale[c, span, :]
             for t in range(tiles):
-                moved = transfer[n * piece : (n + 1) * piece, t * LANES : (t + 1) * LANES]
+                moved = transfer[n * deep : (n + 1) * deep, t * LANES : (t + 1) * LANES]
                 value = totals[n] * field[1 - b, c, t, at, :] + sea_here * moved
                 if step < STEPS - 1:
                     field[1 - b, c, t, at, :] = value
@@ -315,7 +317,8 @@
     weight_load.start()
     for c in edges:
         take_column(c)
-    for k in range(CHUNKS):
+    send_order = list(range(1, CHUNKS - 1)) + [0, CHUNKS - 1]
+    for k in send_order:
         send_lon(0, k)
 
     for copy in small[1:]:
@@ -362,29 +365,37 @@
     weights[...] = jnp.zeros_like(weights)
     weights[0:bins, 0:bins] = raw_weights[...]
 
-    for step in range(STEPS - 1):
-        for k in range(CHUNKS):
-            if k == 0:
-                take_south(step)
-            if k == CHUNKS - 1:
-                take_north(step)
+    for step in range(STEPS):
+        final = step == STEPS - 1
+
+        def rim(k):
             for side in range(2):
                 lon_copy(step, side, k).wait_recv()
             advance(step, k, edges)
-            send_lon(step + 1, k)
-            advance(step, k, inner)
-            if k == 0:
-                send_south(step + 1)
-            if k == CHUNKS - 1:
-                send_north(step + 1)
-    take_south(STEPS - 1)
-    take_north(STEPS - 1)
-    for k in range(CHUNKS):
-        advance(STEPS - 1, k, inner)
-    for k in range(CHUNKS):
-        for side in range(2):
-            lon_copy(STEPS - 1, side, k).wait_recv()
-        advance(STEPS - 1, k, edges)
+            if not final:
+                send_lon(step + 1, k)
+
+        if final:
+            advance(step, 1, inner, CHUNKS - 2)
+        else:
+            for k in range(1, CHUNKS - 1):
+                rim(k)
+            advance(step, 1, inner, CHUNKS - 2)
+        take_south(step)
+        if not final:
+            rim(0)
+        advance(step, 0, inner)
+        if not final:
+            send_south(step + 1)
+        take_north(step)
+        if not final:
+            rim(CHUNKS - 1)
+        advance(step, CHUNKS - 1, inner)
+        if not final:
+            send_north(step + 1)
+        else:
+            for k in send_order:
+                rim(k)
     for step in range(STEPS):
         for k in range(CHUNKS):
             for side in range(2):
@@ -423,7 +434,7 @@
             pltpu.VMEM((columns, rows, bins), f32),
             pltpu.VMEM((wide, wide), jnp.bfloat16),
             pltpu.VMEM((bins, bins), jnp.bfloat16),
-            pltpu.VMEM(((columns - 2) * piece, wide), jnp.bfloat16),
+            pltpu.VMEM(((columns - 2) * piece * 2, wide), jnp.bfloat16),
             pltpu.VMEM((tiles, rows, LANES), f32),
             pltpu.VMEM((tiles, rows, LANES), f32),
             pltpu.VMEM((tiles, 8, LANES), f32),

time: 25.3 us -> 25.2 us (level)
  no operation moved by 1% of the time
where the time goes in v5:
time: 25.2 us; the launch traced here: 25 us
  Pallas kernels  23.8 us (94%)
  local copies, waits for them, and re-layouts  1.15 us (5%)
    pallas_call x1, Pallas kernels, on_device(): pl.pallas_call(functools.partial(kernel, group_speed.shape[0]), out_shape...  23.8 us
    unnamed x1, local copies, waits for them, and re-layouts  1.15 us

profile of v5, /device:TPU:0, one launch (start us, length us, event | category | flops | bytes accessed | tf_op | source)
XLA Modules:
  0.0 25.0 jit_solution(5099579205041463318)
XLA Ops:
  0.0 23.8 %shard_map.64 = f32[8,64,648]{2,1,0:T(8,128)S(1)} custom-call(f32[18]{0:T(128)} %speed_hbm.1, s32[8,64]{1,0:T(8,128)} %sea_hbm.1, s32[8,64]{1,0:T(8,128)} %ice_hbm.1, f32[8,64]{1,0:T(8,128)} %wind_hbm.1, f32[8,64,648]{2,1,0:T(8,128)} %spectrum_ref.1, bf16[648,648]{1,0:T(8,128)(2,1)} %coupling_ref.1), custom_call_target="tpu_custom_call" | custom-call | tf_op jit(solution)/shard_map/pallas_call | solution.py:423
  23.9 1.1 %copy.8 = f32[8,64,648]{2,1,0:T(8,128)} copy(f32[8,64,648]{2,1,0:T(8,128)S(1)} %shard_map.64) | data formatting | bytes 2654208
